TPU v7x, 16 devices: a 4x2x1 block of a 4x4x8 slice. The times are simulated.
16 devices in a mesh: dp: 2 (over y, z), cp: 8 (over x, core).
Axes of the slice: x: 4, y: 2, z: 1, core: 2. Of those that a mesh axis runs over, the one named last changes fastest.
The devices are a block of a 4x4x8 slice.
Arguments:
- x: bfloat16 [4096, 4096], P(('dp', 'cp')), parts along dimension 0
- k_cache: bfloat16 [32768, 8, 128], P(('dp', 'cp')), parts along dimension 0
- v_cache: bfloat16 [32768, 8, 128], P(('dp', 'cp')), parts along dimension 0
- ln_gain: bfloat16 [4096], replicated
- w_q: bfloat16 [4096, 4096], replicated
- w_k: bfloat16 [4096, 1024], replicated
- w_v: bfloat16 [4096, 1024], replicated
- w_o: bfloat16 [4096, 4096], replicated
- q_gain: bfloat16 [128], replicated
- k_gain: bfloat16 [128], replicated
Outputs:
- output 1: bfloat16 [4096, 4096], P(('dp', 'cp')), parts along dimension 0
- output 2: bfloat16 [4096, 8, 128], P(('dp', 'cp')), parts along dimension 0
- output 3: bfloat16 [4096, 8, 128], P(('dp', 'cp')), parts along dimension 0
There are 2 independent parts. A program takes and returns all parts, laid end to end along the dimension named above; an argument that names none is the same for every part.
All inputs are finite; a program needn't handle non-finite values.
Results may differ from a plain program's by a relative error of at most 0.0118422.
Values are sent between devices in bfloat16 or wider.
A program may use at most 768 MiB of HBM per device.

v0:
```python
import jax
import jax.numpy as jnp
from jax import lax
from jax.sharding import PartitionSpec as P

HEAD_DIM = 128
ROPE_THETA = 1.0e6
NORM_EPS = 1.0e-6
MASK_VALUE = -1.0e30


def rms_norm(vals, gain):
    mean_sq = jnp.mean(vals * vals, axis=-1, keepdims=True)
    return vals * lax.rsqrt(mean_sq + NORM_EPS) * gain


def apply_rope(vals, positions):
    half = HEAD_DIM // 2
    inv_freq = ROPE_THETA ** (-jnp.arange(half, dtype=jnp.float32) * (2.0 / HEAD_DIM))
    angles = positions.astype(jnp.float32)[:, None] * inv_freq[None, :]
    cos_tab = jnp.cos(angles)[:, None, :]
    sin_tab = jnp.sin(angles)[:, None, :]
    first = vals[..., :half]
    second = vals[..., half:]
    return jnp.concatenate([first * cos_tab - second * sin_tab, second * cos_tab + first * sin_tab], axis=-1)


def project_rows(x_wide, ln_gain, w_q, w_k, w_v, q_gain, k_gain, positions):
    rows = x_wide.shape[0]
    hidden = rms_norm(x_wide, ln_gain.astype(jnp.float32)).astype(jnp.bfloat16)
    q_raw = jnp.dot(hidden, w_q, preferred_element_type=jnp.float32).astype(jnp.bfloat16).reshape(rows, -1, HEAD_DIM)
    k_raw = jnp.dot(hidden, w_k, preferred_element_type=jnp.float32).astype(jnp.bfloat16).reshape(rows, -1, HEAD_DIM)
    v_new = jnp.dot(hidden, w_v, preferred_element_type=jnp.float32).astype(jnp.bfloat16).reshape(rows, -1, HEAD_DIM)
    q_rot = apply_rope(rms_norm(q_raw.astype(jnp.float32), q_gain.astype(jnp.float32)), positions).astype(jnp.bfloat16)
    k_new = apply_rope(rms_norm(k_raw.astype(jnp.float32), k_gain.astype(jnp.float32)), positions).astype(jnp.bfloat16)
    return q_rot, k_new, v_new


def partial_attend(q_grp, keys, vals, allowed):
    scale = HEAD_DIM ** -0.5
    scores = jnp.einsum('rkgd,skd->krgs', q_grp, keys, preferred_element_type=jnp.float32) * scale
    if allowed is not None:
        scores = jnp.where(allowed[None, :, None, :], scores, MASK_VALUE)
    peak = jnp.max(scores, axis=-1)
    weights = jnp.exp(scores - peak[..., None])
    weighted = jnp.einsum('krgs,skd->krgd', weights.astype(jnp.bfloat16), vals, preferred_element_type=jnp.float32)
    return peak, jnp.sum(weights, axis=-1), weighted


def combine_two(first, second):
    peak_a, sum_a, acc_a = first
    peak_b, sum_b, acc_b = second
    top_peak = jnp.maximum(jnp.max(peak_a, axis=0), jnp.max(peak_b, axis=0))
    factor_a = jnp.exp(peak_a - top_peak[None])
    factor_b = jnp.exp(peak_b - top_peak[None])
    total_sum = jnp.sum(factor_a * sum_a, axis=0) + jnp.sum(factor_b * sum_b, axis=0)
    total = jnp.sum(factor_a[..., None] * acc_a, axis=0) + jnp.sum(factor_b[..., None] * acc_b, axis=0)
    return total / total_sum[..., None]


def solution(mesh):
    cp_size = mesh.shape['cp']
    row_spec = P(('dp', 'cp'), None)
    cache_spec = P(('dp', 'cp'), None, None)
    whole = P()

    def device_step(x_rows, k_cache, v_cache, ln_gain, w_q, w_k, w_v, w_o, q_gain, k_gain):
        rows = x_rows.shape[0]
        prefix_len = k_cache.shape[0] * cp_size
        kv_heads = k_cache.shape[1]
        q_heads = w_q.shape[1] // HEAD_DIM
        group = q_heads // kv_heads
        my_index = lax.axis_index('cp')
        row_ids = my_index * rows + jnp.arange(rows)
        key_ids = jnp.arange(rows)
        x_wide = x_rows.astype(jnp.float32)
        q_rot, k_new, v_new = project_rows(x_wide, ln_gain, w_q, w_k, w_v, q_gain, k_gain, prefix_len + row_ids)
        q_grp = q_rot.reshape(rows, kv_heads, group, HEAD_DIM)
        every_q = lax.all_gather(q_grp, 'cp')
        every_k = lax.all_gather(k_new, 'cp')
        every_v = lax.all_gather(v_new, 'cp')

        def block_work(block):
            q_block, k_block, v_block, source = block
            prefix_part = partial_attend(q_block, k_cache, v_cache, None)
            allowed = (source * rows + key_ids)[None, :] <= row_ids[:, None]
            new_part = partial_attend(q_grp, k_block, v_block, allowed)
            return prefix_part, new_part

        prefix_parts, new_parts = lax.map(block_work, (every_q, every_k, every_v, jnp.arange(cp_size)))
        returned = tuple(lax.all_to_all(piece, 'cp', 0, 0, tiled=True) for piece in prefix_parts)
        attended = combine_two(returned, new_parts)
        attended = jnp.transpose(attended, (1, 0, 2, 3)).reshape(rows, q_heads * HEAD_DIM).astype(jnp.bfloat16)
        out = (x_wide + jnp.dot(attended, w_o, preferred_element_type=jnp.float32)).astype(jnp.bfloat16)
        return out, k_new, v_new

    return jax.shard_map(device_step, mesh=mesh, in_specs=(row_spec, cache_spec, cache_spec, whole, whole, whole, whole, whole, whole, whole), out_specs=(row_spec, cache_spec, cache_spec), check_vma=False)
```

profile of v0, /device:TPU:113, one launch (start us, length us, event | category | flops | bytes accessed | tf_op | source)
XLA Modules:
  0.0 1276.9 jit_solution(8851416751908850990)
XLA Ops:
  80.8 80.5 %all-gather.4.cloned.1.call-done = bf16[8,256,8,4,128]{4,2,3,1,0:T(8,128)(2,1)} async-done(((bf16[1,256,8,4,128]{4,2,3,1,0:T(8,128)(2,1)}), bf16[8,256,8,4,128]{4,2,3,1,0:T(8,128)(2,1)}) %all-gather.4.cloned.1.call-update) | async-done | bytes 16777232 | tf_op jit(solution)/shard_map/all_gather | solution.py:79
  161.3 678.4 %while.21 = (s32[]{:T(128)}, f32[8,8,256,4]{2,3,1,0:T(4,128)S(1)}, f32[8,8,256,4]{2,3,1,0:T(4,128)S(1)}, f32[8,8,256,4,128]{4,2,3,1,0:T(8,128)}, f32[8,8,256,4]{...) while((s32[]{:T(128)}, f32[8,8,256,4]{2,3,1,0:T(4,128)S(1)}, ...), condition=%wide.region_8.9_spmd.clone, body=%wide.region_3.8_spmd.clone.sunk | while | flops 9820995584 | bytes 289149216 | solution.py:90
  174.7 23.1 %multiply_reduce_fusion.8 = (f32[8,256,4]{1,2,0:T(4,128)S(1)}, f32[8,256,4,2048]{3,1,2,0:T(8,128)}) fusion(bf16[2048,8,128]{2,0,1:T(8,128)(2,1)S(1)} %copy-done, bf16[1,256,8,4,128]{4,2,3,1,0:T(8,128)(2,1)S(1)} %constant_dynamic-slice_fusion.6), kind=kOutput, calls=%fused_computation.3.clone.1 | convolution fusion | flops 4328513536 | bytes 73433088 | tf_op jit(solution)/shard_map/while/body/eval_jaxpr/rkgd,skd->krgs/dot_general | solution.py:41
  197.9 21.2 %fusion.60 = f32[8,256,4]{1,2,0:T(4,128)S(1)} fusion(f32[8,256,4,2048]{3,1,2,0:T(8,128)} %get-tuple-element.384, f32[8,256,4]{1,2,0:T(4,128)S(1)} %get-tuple-element.385), kind=kLoop, calls=%fused_computation.5.clone.1 | loop fusion | flops 50323456 | bytes 67174400 | tf_op jit(solution)/shard_map/while/body/eval_jaxpr/reduce_sum | solution.py:47
  219.1 27.0 %bitcast_dynamic-update-slice_fusion.11 = f32[8,8,256,4,128]{4,2,3,1,0:T(8,128)} fusion(f32[8,8,256,4,128]{4,2,3,1,0:T(8,128)} %get-tuple-element.412, s32[]{:T(128)S(6)} %copy.139, bf16[2048,8,128]{2,0,1:T(8,128)(2,1)} %get-tuple-element.435, f32[8,256,4,2048]{3,1,2,0:T(8,128)} %get-tuple-element.384, f32[8,256,4]{1,2,0:T(4,128)S(1)} %get-tuple-element.385), kind=kOutput, calls=%fused_computation.17.clone.1 | convolution fusion | flops 4345298944 | bytes 75530240 | tf_op jit(solution)/shard_map/while/body/eval_jaxpr/krgs,skd->krgd/dot_general | solution.py:46
  259.6 23.1 %multiply_reduce_fusion.8 = (f32[8,256,4]{1,2,0:T(4,128)S(1)}, f32[8,256,4,2048]{3,1,2,0:T(8,128)}) fusion(bf16[2048,8,128]{2,0,1:T(8,128)(2,1)S(1)} %copy-done, bf16[1,256,8,4,128]{4,2,3,1,0:T(8,128)(2,1)S(1)} %constant_dynamic-slice_fusion.6), kind=kOutput, calls=%fused_computation.3.clone.1 | convolution fusion | flops 4328513536 | bytes 73433088 | tf_op jit(solution)/shard_map/while/body/eval_jaxpr/rkgd,skd->krgs/dot_general | solution.py:41
  282.7 21.2 %fusion.60 = f32[8,256,4]{1,2,0:T(4,128)S(1)} fusion(f32[8,256,4,2048]{3,1,2,0:T(8,128)} %get-tuple-element.384, f32[8,256,4]{1,2,0:T(4,128)S(1)} %get-tuple-element.385), kind=kLoop, calls=%fused_computation.5.clone.1 | loop fusion | flops 50323456 | bytes 67174400 | tf_op jit(solution)/shard_map/while/body/eval_jaxpr/reduce_sum | solution.py:47
  303.9 27.0 %bitcast_dynamic-update-slice_fusion.11 = f32[8,8,256,4,128]{4,2,3,1,0:T(8,128)} fusion(f32[8,8,256,4,128]{4,2,3,1,0:T(8,128)} %get-tuple-element.412, s32[]{:T(128)S(6)} %copy.139, bf16[2048,8,128]{2,0,1:T(8,128)(2,1)} %get-tuple-element.435, f32[8,256,4,2048]{3,1,2,0:T(8,128)} %get-tuple-element.384, f32[8,256,4]{1,2,0:T(4,128)S(1)} %get-tuple-element.385), kind=kOutput, calls=%fused_computation.17.clone.1 | convolution fusion | flops 4345298944 | bytes 75530240 | tf_op jit(solution)/shard_map/while/body/eval_jaxpr/krgs,skd->krgd/dot_general | solution.py:46
  344.3 23.1 %multiply_reduce_fusion.8 = (f32[8,256,4]{1,2,0:T(4,128)S(1)}, f32[8,256,4,2048]{3,1,2,0:T(8,128)}) fusion(bf16[2048,8,128]{2,0,1:T(8,128)(2,1)S(1)} %copy-done, bf16[1,256,8,4,128]{4,2,3,1,0:T(8,128)(2,1)S(1)} %constant_dynamic-slice_fusion.6), kind=kOutput, calls=%fused_computation.3.clone.1 | convolution fusion | flops 4328513536 | bytes 73433088 | tf_op jit(solution)/shard_map/while/body/eval_jaxpr/rkgd,skd->krgs/dot_general | solution.py:41
  367.4 21.2 %fusion.60 = f32[8,256,4]{1,2,0:T(4,128)S(1)} fusion(f32[8,256,4,2048]{3,1,2,0:T(8,128)} %get-tuple-element.384, f32[8,256,4]{1,2,0:T(4,128)S(1)} %get-tuple-element.385), kind=kLoop, calls=%fused_computation.5.clone.1 | loop fusion | flops 50323456 | bytes 67174400 | tf_op jit(solution)/shard_map/while/body/eval_jaxpr/reduce_sum | solution.py:47
  388.6 27.1 %bitcast_dynamic-update-slice_fusion.11 = f32[8,8,256,4,128]{4,2,3,1,0:T(8,128)} fusion(f32[8,8,256,4,128]{4,2,3,1,0:T(8,128)} %get-tuple-element.412, s32[]{:T(128)S(6)} %copy.139, bf16[2048,8,128]{2,0,1:T(8,128)(2,1)} %get-tuple-element.435, f32[8,256,4,2048]{3,1,2,0:T(8,128)} %get-tuple-element.384, f32[8,256,4]{1,2,0:T(4,128)S(1)} %get-tuple-element.385), kind=kOutput, calls=%fused_computation.17.clone.1 | convolution fusion | flops 4345298944 | bytes 75530240 | tf_op jit(solution)/shard_map/while/body/eval_jaxpr/krgs,skd->krgd/dot_general | solution.py:46
  429.0 23.1 %multiply_reduce_fusion.8 = (f32[8,256,4]{1,2,0:T(4,128)S(1)}, f32[8,256,4,2048]{3,1,2,0:T(8,128)}) fusion(bf16[2048,8,128]{2,0,1:T(8,128)(2,1)S(1)} %copy-done, bf16[1,256,8,4,128]{4,2,3,1,0:T(8,128)(2,1)S(1)} %constant_dynamic-slice_fusion.6), kind=kOutput, calls=%fused_computation.3.clone.1 | convolution fusion | flops 4328513536 | bytes 73433088 | tf_op jit(solution)/shard_map/while/body/eval_jaxpr/rkgd,skd->krgs/dot_general | solution.py:41
  452.1 21.2 %fusion.60 = f32[8,256,4]{1,2,0:T(4,128)S(1)} fusion(f32[8,256,4,2048]{3,1,2,0:T(8,128)} %get-tuple-element.384, f32[8,256,4]{1,2,0:T(4,128)S(1)} %get-tuple-element.385), kind=kLoop, calls=%fused_computation.5.clone.1 | loop fusion | flops 50323456 | bytes 67174400 | tf_op jit(solution)/shard_map/while/body/eval_jaxpr/reduce_sum | solution.py:47
  473.3 27.1 %bitcast_dynamic-update-slice_fusion.11 = f32[8,8,256,4,128]{4,2,3,1,0:T(8,128)} fusion(f32[8,8,256,4,128]{4,2,3,1,0:T(8,128)} %get-tuple-element.412, s32[]{:T(128)S(6)} %copy.139, bf16[2048,8,128]{2,0,1:T(8,128)(2,1)} %get-tuple-element.435, f32[8,256,4,2048]{3,1,2,0:T(8,128)} %get-tuple-element.384, f32[8,256,4]{1,2,0:T(4,128)S(1)} %get-tuple-element.385), kind=kOutput, calls=%fused_computation.17.clone.1 | convolution fusion | flops 4345298944 | bytes 75530240 | tf_op jit(solution)/shard_map/while/body/eval_jaxpr/krgs,skd->krgd/dot_general | solution.py:46
  513.7 23.1 %multiply_reduce_fusion.8 = (f32[8,256,4]{1,2,0:T(4,128)S(1)}, f32[8,256,4,2048]{3,1,2,0:T(8,128)}) fusion(bf16[2048,8,128]{2,0,1:T(8,128)(2,1)S(1)} %copy-done, bf16[1,256,8,4,128]{4,2,3,1,0:T(8,128)(2,1)S(1)} %constant_dynamic-slice_fusion.6), kind=kOutput, calls=%fused_computation.3.clone.1 | convolution fusion | flops 4328513536 | bytes 73433088 | tf_op jit(solution)/shard_map/while/body/eval_jaxpr/rkgd,skd->krgs/dot_general | solution.py:41
  536.8 21.2 %fusion.60 = f32[8,256,4]{1,2,0:T(4,128)S(1)} fusion(f32[8,256,4,2048]{3,1,2,0:T(8,128)} %get-tuple-element.384, f32[8,256,4]{1,2,0:T(4,128)S(1)} %get-tuple-element.385), kind=kLoop, calls=%fused_computation.5.clone.1 | loop fusion | flops 50323456 | bytes 67174400 | tf_op jit(solution)/shard_map/while/body/eval_jaxpr/reduce_sum | solution.py:47
  558.1 27.0 %bitcast_dynamic-update-slice_fusion.11 = f32[8,8,256,4,128]{4,2,3,1,0:T(8,128)} fusion(f32[8,8,256,4,128]{4,2,3,1,0:T(8,128)} %get-tuple-element.412, s32[]{:T(128)S(6)} %copy.139, bf16[2048,8,128]{2,0,1:T(8,128)(2,1)} %get-tuple-element.435, f32[8,256,4,2048]{3,1,2,0:T(8,128)} %get-tuple-element.384, f32[8,256,4]{1,2,0:T(4,128)S(1)} %get-tuple-element.385), kind=kOutput, calls=%fused_computation.17.clone.1 | convolution fusion | flops 4345298944 | bytes 75530240 | tf_op jit(solution)/shard_map/while/body/eval_jaxpr/krgs,skd->krgd/dot_general | solution.py:46
  598.5 23.1 %multiply_reduce_fusion.8 = (f32[8,256,4]{1,2,0:T(4,128)S(1)}, f32[8,256,4,2048]{3,1,2,0:T(8,128)}) fusion(bf16[2048,8,128]{2,0,1:T(8,128)(2,1)S(1)} %copy-done, bf16[1,256,8,4,128]{4,2,3,1,0:T(8,128)(2,1)S(1)} %constant_dynamic-slice_fusion.6), kind=kOutput, calls=%fused_computation.3.clone.1 | convolution fusion | flops 4328513536 | bytes 73433088 | tf_op jit(solution)/shard_map/while/body/eval_jaxpr/rkgd,skd->krgs/dot_general | solution.py:41
  642.9 27.0 %bitcast_dynamic-update-slice_fusion.11 = f32[8,8,256,4,128]{4,2,3,1,0:T(8,128)} fusion(f32[8,8,256,4,128]{4,2,3,1,0:T(8,128)} %get-tuple-element.412, s32[]{:T(128)S(6)} %copy.139, bf16[2048,8,128]{2,0,1:T(8,128)(2,1)} %get-tuple-element.435, f32[8,256,4,2048]{3,1,2,0:T(8,128)} %get-tuple-element.384, f32[8,256,4]{1,2,0:T(4,128)S(1)} %get-tuple-element.385), kind=kOutput, calls=%fused_computation.17.clone.1 | convolution fusion | flops 4345298944 | bytes 75530240 | tf_op jit(solution)/shard_map/while/body/eval_jaxpr/krgs,skd->krgd/dot_general | solution.py:46
  683.2 23.1 %multiply_reduce_fusion.8 = (f32[8,256,4]{1,2,0:T(4,128)S(1)}, f32[8,256,4,2048]{3,1,2,0:T(8,128)}) fusion(bf16[2048,8,128]{2,0,1:T(8,128)(2,1)S(1)} %copy-done, bf16[1,256,8,4,128]{4,2,3,1,0:T(8,128)(2,1)S(1)} %constant_dynamic-slice_fusion.6), kind=kOutput, calls=%fused_computation.3.clone.1 | convolution fusion | flops 4328513536 | bytes 73433088 | tf_op jit(solution)/shard_map/while/body/eval_jaxpr/rkgd,skd->krgs/dot_general | solution.py:41
  727.6 27.1 %bitcast_dynamic-update-slice_fusion.11 = f32[8,8,256,4,128]{4,2,3,1,0:T(8,128)} fusion(f32[8,8,256,4,128]{4,2,3,1,0:T(8,128)} %get-tuple-element.412, s32[]{:T(128)S(6)} %copy.139, bf16[2048,8,128]{2,0,1:T(8,128)(2,1)} %get-tuple-element.435, f32[8,256,4,2048]{3,1,2,0:T(8,128)} %get-tuple-element.384, f32[8,256,4]{1,2,0:T(4,128)S(1)} %get-tuple-element.385), kind=kOutput, calls=%fused_computation.17.clone.1 | convolution fusion | flops 4345298944 | bytes 75530240 | tf_op jit(solution)/shard_map/while/body/eval_jaxpr/krgs,skd->krgd/dot_general | solution.py:46
  767.9 23.1 %multiply_reduce_fusion.8 = (f32[8,256,4]{1,2,0:T(4,128)S(1)}, f32[8,256,4,2048]{3,1,2,0:T(8,128)}) fusion(bf16[2048,8,128]{2,0,1:T(8,128)(2,1)S(1)} %copy-done, bf16[1,256,8,4,128]{4,2,3,1,0:T(8,128)(2,1)S(1)} %constant_dynamic-slice_fusion.6), kind=kOutput, calls=%fused_computation.3.clone.1 | convolution fusion | flops 4328513536 | bytes 73433088 | tf_op jit(solution)/shard_map/while/body/eval_jaxpr/rkgd,skd->krgs/dot_general | solution.py:41
  812.3 27.1 %bitcast_dynamic-update-slice_fusion.11 = f32[8,8,256,4,128]{4,2,3,1,0:T(8,128)} fusion(f32[8,8,256,4,128]{4,2,3,1,0:T(8,128)} %get-tuple-element.412, s32[]{:T(128)S(6)} %copy.139, bf16[2048,8,128]{2,0,1:T(8,128)(2,1)} %get-tuple-element.435, f32[8,256,4,2048]{3,1,2,0:T(8,128)} %get-tuple-element.384, f32[8,256,4]{1,2,0:T(4,128)S(1)} %get-tuple-element.385), kind=kOutput, calls=%fused_computation.17.clone.1 | convolution fusion | flops 4345298944 | bytes 75530240 | tf_op jit(solution)/shard_map/while/body/eval_jaxpr/krgs,skd->krgd/dot_general | solution.py:46
  883.9 347.5 %all-to-all-done.1 = f32[8,8,256,4,128]{4,2,3,1,0:T(8,128)} async-done(((f32[8,8,256,4,128]{4,2,3,1,0:T(8,128)}), f32[8,8,256,4,128]{4,2,3,1,0:T(8,128)}, u32[]{:S(2)}, u32[]{:S(2)}) %all-to-all-start.1) | async-done | bytes 33554464 | tf_op jit(solution)/shard_map/all_to_all | solution.py:91
  (238 shorter events, 320.2 us)
Async XLA Ops:
  7.2 73.6 %all-gather.8.cloned.1.call-start = ((), (), s32[]{:S(2)}) async-start(), calls=%async_computation.5 | async-start | bytes 4718592 | tf_op jit(solution)/shard_map/all_gather | solution.py:81
  9.3 10.1 copy-start.14
  10.1 9.4 copy-start.12
  10.1 7.6 copy-start.15
  10.1 9.4 copy-start.4
  17.6 63.3 %all-gather.6.cloned.1.call-start = ((), (), s32[]{:S(2)}) async-start(), calls=%async_computation.4 | async-start | bytes 4718592 | tf_op jit(solution)/shard_map/all_gather | solution.py:80
  30.5 130.7 %all-gather.4.cloned.1.call-start = ((), (), s32[]{:S(2)}) async-start(), calls=%async_computation.3 | async-start | bytes 18874368 | tf_op jit(solution)/shard_map/all_gather | solution.py:79
  161.5 7.1 copy-start.1
  219.1 27.1 %copy-start.2 = (bf16[256,8,4,128]{3,0,2,1:T(8,128)(2,1)S(1)}, bf16[256,8,4,128]{3,0,2,1:T(8,128)(2,1)}, u32[]{:S(2)}) copy-start(bf16[256,8,4,128]{3,0,2,1:T(8,128)(2,1)} %copy-done.1) | copy-start | bytes 6291460 | tf_op jit(solution)/shard_map/while
  246.2 7.1 copy-start.1
  303.9 27.1 %copy-start.2 = (bf16[256,8,4,128]{3,0,2,1:T(8,128)(2,1)S(1)}, bf16[256,8,4,128]{3,0,2,1:T(8,128)(2,1)}, u32[]{:S(2)}) copy-start(bf16[256,8,4,128]{3,0,2,1:T(8,128)(2,1)} %copy-done.1) | copy-start | bytes 6291460 | tf_op jit(solution)/shard_map/while
  331.0 7.1 copy-start.1
  388.6 27.1 %copy-start.2 = (bf16[256,8,4,128]{3,0,2,1:T(8,128)(2,1)S(1)}, bf16[256,8,4,128]{3,0,2,1:T(8,128)(2,1)}, u32[]{:S(2)}) copy-start(bf16[256,8,4,128]{3,0,2,1:T(8,128)(2,1)} %copy-done.1) | copy-start | bytes 6291460 | tf_op jit(solution)/shard_map/while
  473.3 27.1 %copy-start.2 = (bf16[256,8,4,128]{3,0,2,1:T(8,128)(2,1)S(1)}, bf16[256,8,4,128]{3,0,2,1:T(8,128)(2,1)}, u32[]{:S(2)}) copy-start(bf16[256,8,4,128]{3,0,2,1:T(8,128)(2,1)} %copy-done.1) | copy-start | bytes 6291460 | tf_op jit(solution)/shard_map/while
  500.5 7.1 copy-start.1
  558.1 27.1 %copy-start.2 = (bf16[256,8,4,128]{3,0,2,1:T(8,128)(2,1)S(1)}, bf16[256,8,4,128]{3,0,2,1:T(8,128)(2,1)}, u32[]{:S(2)}) copy-start(bf16[256,8,4,128]{3,0,2,1:T(8,128)(2,1)} %copy-done.1) | copy-start | bytes 6291460 | tf_op jit(solution)/shard_map/while
  642.9 27.1 %copy-start.2 = (bf16[256,8,4,128]{3,0,2,1:T(8,128)(2,1)S(1)}, bf16[256,8,4,128]{3,0,2,1:T(8,128)(2,1)}, u32[]{:S(2)}) copy-start(bf16[256,8,4,128]{3,0,2,1:T(8,128)(2,1)} %copy-done.1) | copy-start | bytes 6291460 | tf_op jit(solution)/shard_map/while
  727.6 27.1 %copy-start.2 = (bf16[256,8,4,128]{3,0,2,1:T(8,128)(2,1)S(1)}, bf16[256,8,4,128]{3,0,2,1:T(8,128)(2,1)}, u32[]{:S(2)}) copy-start(bf16[256,8,4,128]{3,0,2,1:T(8,128)(2,1)} %copy-done.1) | copy-start | bytes 6291460 | tf_op jit(solution)/shard_map/while
  754.7 7.1 copy-start.1
  812.3 27.1 %copy-start.2 = (bf16[256,8,4,128]{3,0,2,1:T(8,128)(2,1)S(1)}, bf16[256,8,4,128]{3,0,2,1:T(8,128)(2,1)}, u32[]{:S(2)}) copy-start(bf16[256,8,4,128]{3,0,2,1:T(8,128)(2,1)} %copy-done.1) | copy-start | bytes 6291460 | tf_op jit(solution)/shard_map/while
  859.9 8.2 copy-start.8
  859.9 8.2 copy-start.10
  860.0 371.5 %all-to-all-start.1 = ((f32[8,8,256,4,128]{4,2,3,1,0:T(8,128)}), f32[8,8,256,4,128]{4,2,3,1,0:T(8,128)}, u32[]{:S(2)}, u32[]{:S(2)}) async-start(f32[8,8,256,4,128]{4,2,3,1,0:T(8,128)} %get-tuple-element.92), calls=%async_computation.1 | async-start | bytes 67108864 | tf_op jit(solution)/shard_map/all_to_all | solution.py:91
  1231.4 14.3 %copy-start.3 = (f32[8,256,4,128]{3,1,2,0:T(8,128)S(1)}, f32[8,256,4,128]{3,1,2,0:T(8,128)}, u32[]{:S(2)}) copy-start(f32[8,256,4,128]{3,1,2,0:T(8,128)} %multiply_reduce_fusion.1) | copy-start | bytes 12582916
  (17 other events, 74.3 us)
Sparse Core Ops, SparseCore 0:
  17.7 31.0 all-gather.7
  50.9 27.6 all-gather.5
  80.2 80.9 all-gather.3
where the time goes:
time: 1280 us
  matrix products  492 us (38%)
  waiting for transfers between devices  428 us (33%)
  other arithmetic  237 us (19%)
  local copies, waits for them, and re-layouts  69.3 us (5%)
  blocking collectives  20.3 us (2%)
  between operations  14.5 us (1%)
    all_to_all x1, waiting for transfers between devices, device_step(): lax.all_to_all(piece, 'cp', 0, 0, tiled=True)  348 us
    dot_general x16, matrix products, partial_attend(): jnp.einsum('krgs,skd->krgd', weights.astype(jnp.bfloat16), vals, preferre...  251 us
    dot_general x16, matrix products, partial_attend(): jnp.einsum('rkgd,skd->krgs', q_grp, keys, preferred_element_type=jnp.floa...  196 us
    reduce_sum x16, other arithmetic, partial_attend(): return (peak, jnp.sum(weights, axis=-1), weighted)  185 us
    all_gather x1, waiting for transfers between devices, device_step(): every_q = lax.all_gather(q_grp, 'cp')  80.5 us
    dynamic_slice x32, local copies, waits for them, and re-layouts, device_step(): lax.map(block_work, (every_q, every_k, every_v, jnp.arange(cp_size)))  38.4 us
  transfers between devices with their start and end apart: 4, of which 2 were waited for; matrix products, arithmetic and copies ran while one was open for 6% of the time, Pallas kernels for 0%

commit v1 on v0

v1 whole, which is shorter than its diff:
```python
import functools

import jax
import jax.numpy as jnp
from jax import lax
from jax.experimental import pallas as pl
from jax.experimental.pallas import tpu as pltpu
from jax.sharding import PartitionSpec as P

HEAD_DIM = 128
ROPE_THETA = 1.0e6
NORM_EPS = 1.0e-6
SCALE2 = HEAD_DIM ** -0.5 * 1.4426950408889634
KEY_BLOCK = 256
NEW_UNIT = 4
W_SLOTS = 4
W_COLS = 512
MESH = pl.DeviceIdType.MESH
NEG_INF = float('-inf')


def rope_tables(positions):
    half = HEAD_DIM // 2
    inv_freq = ROPE_THETA ** (-jnp.arange(half, dtype=jnp.float32) * (2.0 / HEAD_DIM))
    angles = positions.astype(jnp.float32)[:, None] * inv_freq[None, :]
    cos_tab = jnp.cos(angles)
    sin_tab = jnp.sin(angles)
    return jnp.concatenate([cos_tab, cos_tab], axis=-1), jnp.concatenate([-sin_tab, sin_tab], axis=-1)


def ring_order(n):
    chips = n // 2
    order = [(0, 0), (0, 1)]
    for d in range(1, chips // 2 + 1):
        if 2 * d == chips:
            order += [(d, 0), (d, 1)]
        else:
            order += [(d, 0), (chips - d, 0), (d, 1), (chips - d, 1)]
    return order


def make_kernel(n, rows, cache_rows, group):
    order = ring_order(n)
    chips = n // 2
    qcols = group * HEAD_DIM
    tile_q = 512
    halves = rows * group // tile_q
    tiles = n * halves
    phases = n // 2
    blocks = 2 * cache_rows // KEY_BLOCK
    per_chunk = cache_rows // KEY_BLOCK
    kv_per_tile = W_COLS // HEAD_DIM

    def kernel(x_ref, gain_ref, qg_ref, kg_ref, cos_ref, sin_ref, kc, vc, wq, wk, wv, wo,
               out_ref, kn_ref, vn_ref,
               h_ref, wbuf, kbuf, vbuf, qsend, qbuf, nkbuf, nvsend, nvbuf, osend, obuf,
               s_ref, s2_ref, acc, m_ref, l_ref, mx_ref,
               wsem, lsem, sk, rk, sv, rv, sq, rq, snk, rnk, snv, rnv, so, ro):
        me = lax.axis_index('cp')
        chip = me // 2
        core = me % 2

        def peer(j):
            if isinstance(j, int):
                dc, fl = order[j]
            else:
                dc, fl = jnp.int32(0), jnp.int32(0)
                for i, (a, b) in enumerate(order):
                    dc = jnp.where(j == i, a, dc)
                    fl = jnp.where(j == i, b, fl)
            return ((chip + dc) % chips) * 2 + (core + fl) % 2

        def remote(src, dst, ssem, rsem, dev):
            return pltpu.make_async_remote_copy(src_ref=src, dst_ref=dst, send_sem=ssem, recv_sem=rsem,
                                                device_id={'cp': dev}, device_id_type=MESH)

        def k_copy(dev, who):
            return remote(kc.at[dev], kbuf.at[who], sk.at[dev], rk.at[who], dev)

        def v_copy(dev, who):
            return remote(vc.at[dev], vbuf.at[who], sv.at[dev], rv.at[who], dev)

        def q_copy(dev, who):
            return remote(qsend.at[dev], qbuf.at[who], sq.at[dev], rq.at[who], dev)

        def nk_copy(dev, who):
            return remote(kn_ref.at[dev], nkbuf.at[who], snk.at[dev], rnk.at[who], dev)

        def nv_copy(dev, who):
            return remote(nvsend.at[dev], nvbuf.at[who], snv.at[dev], rnv.at[who], dev)

        def o_copy(dev, who):
            return remote(osend.at[dev], obuf.at[who], so.at[dev], ro.at[who], dev)

        def w_copy(src, col, slot):
            return pltpu.make_async_copy(src.at[:, pl.ds(pl.multiple_of(col * W_COLS, W_COLS), W_COLS)],
                                         wbuf.at[slot], wsem.at[slot])

        def q_dest(t):
            if isinstance(t, int):
                return peer(t + 2 if t < n - 2 else n - 1 - t)
            return peer(jnp.where(t < n - 2, t + 2, n - 1 - t))

        for t in range(W_SLOTS):
            w_copy(wq, q_dest(t), t).start()
        own_k = pltpu.make_async_copy(kc.at[me], kbuf.at[me], lsem.at[0])
        own_v = pltpu.make_async_copy(vc.at[me], vbuf.at[me], lsem.at[1])
        own_k.start()
        own_v.start()

        barrier = pltpu.get_barrier_semaphore()
        for j in range(1, n):
            pl.semaphore_signal(barrier, inc=1, device_id={'cp': peer(j)}, device_id_type=MESH)
        pl.semaphore_wait(barrier, n - 1)

        early = [1, 2, 3]
        late = [j for j in range(1, n) if j not in early]
        for j in early:
            k_copy(peer(j), me).start()
            v_copy(peer(j), me).start()

        gain = gain_ref[...].astype(jnp.float32)

        def norm_rows(r, _):
            sl = pl.ds(pl.multiple_of(r * 16, 16), 16)
            xw = x_ref[sl, :].astype(jnp.float32)
            ms = jnp.mean(xw * xw, axis=-1, keepdims=True)
            h_ref[sl, :] = (xw * lax.rsqrt(ms + NORM_EPS) * gain).astype(jnp.bfloat16)
            return 0

        lax.fori_loop(0, rows // 16, norm_rows, 0)

        def init_tile(t, _):
            acc[t] = jnp.zeros((HEAD_DIM, tile_q), jnp.float32)
            m_ref[t] = jnp.full((8, tile_q), NEG_INF, jnp.float32)
            l_ref[t] = jnp.zeros((8, tile_q), jnp.float32)
            return 0

        lax.fori_loop(0, tiles, init_tile, 0)

        def project(slot):
            return jnp.dot(h_ref[...], wbuf[slot], preferred_element_type=jnp.float32).astype(jnp.bfloat16)

        def norm_rope(raw, head_gain):
            val = raw.astype(jnp.float32)
            ms = jnp.mean(val * val, axis=-1, keepdims=True)
            val = val * lax.rsqrt(ms + NORM_EPS) * head_gain
            return (val * cos_ref[...] + pltpu.roll(val, HEAD_DIM // 2, 1) * sin_ref[...]).astype(jnp.bfloat16)

        q_gain = qg_ref[...].astype(jnp.float32)
        k_gain = kg_ref[...].astype(jnp.float32)
        k_tiles = n // kv_per_tile

        def q_tile(t, _):
            slot = t % W_SLOTS
            dest = q_dest(t)
            w_copy(wq, dest, slot).wait()
            y = project(slot)
            for g in range(group):
                qsend[dest, pl.ds(g * rows, rows), :] = norm_rope(y[:, g * HEAD_DIM:(g + 1) * HEAD_DIM], q_gain)

            @pl.when(t < n - W_SLOTS)
            def _():
                w_copy(wq, q_dest(t + W_SLOTS), slot).start()

            for i in range(k_tiles):
                @pl.when(t == n - W_SLOTS + i)
                def _(i=i):
                    w_copy(wk, i, slot).start()

                @pl.when(t == n - W_SLOTS + k_tiles + i)
                def _(i=i):
                    w_copy(wv, i, slot).start()

            @pl.when(t < n - 1)
            def _():
                q_copy(dest, me).start()

            return 0

        lax.fori_loop(0, n, q_tile, 0)
        qbuf[me] = qsend[me]

        def k_tile(t, _):
            slot = (n + t) % W_SLOTS
            w_copy(wk, t, slot).wait()
            y = project(slot)
            for g in range(kv_per_tile):
                kn_ref[t * kv_per_tile + g] = norm_rope(y[:, g * HEAD_DIM:(g + 1) * HEAD_DIM], k_gain)
            w_copy(wo, t, slot).start()
            return 0

        lax.fori_loop(0, k_tiles, k_tile, 0)
        nkbuf[me] = kn_ref[me]

        def v_tile(t, _):
            slot = (n + k_tiles + t) % W_SLOTS
            w_copy(wv, t, slot).wait()
            y = project(slot)
            for g in range(kv_per_tile):
                val = y[:, g * HEAD_DIM:(g + 1) * HEAD_DIM]
                vn_ref[t * kv_per_tile + g] = val
                nvsend[t * kv_per_tile + g] = val.T
            w_copy(wo, k_tiles + t, slot).start()
            return 0

        lax.fori_loop(0, k_tiles, v_tile, 0)
        nvbuf[me] = nvsend[me]

        for j in late[:2]:
            k_copy(peer(j), me).start()
            v_copy(peer(j), me).start()
        for j in range(1, n):
            nk_copy(peer(j), me).start()
            nv_copy(peer(j), me).start()
        for j in late[2:]:
            k_copy(peer(j), me).start()
            v_copy(peer(j), me).start()

        def block_index(p, t):
            i = t // halves
            return jnp.where(p == phases - 1, n - 1 - i, i)

        def q_of(src, hf):
            return qbuf[src, pl.ds(pl.multiple_of(hf * tile_q, tile_q), tile_q), :]

        def qk(b, chunks, q):
            kk = kbuf[chunks[b // per_chunk], (b % per_chunk) * KEY_BLOCK:(b % per_chunk + 1) * KEY_BLOCK, :]
            s = lax.dot_general(kk, q, (((1,), (1,)), ((), ())), preferred_element_type=jnp.float32)
            s_ref[b * KEY_BLOCK:(b + 1) * KEY_BLOCK, :] = s
            return jnp.max(s.reshape(KEY_BLOCK // 8, 8, tile_q), axis=0)

        def fold(total, term, op):
            return term if total is None else op(total, term)

        def step(slot, chunks, next_chunks, next_q):
            m_old = m_ref[slot]
            m_new = jnp.maximum(m_old, jnp.max(mx_ref[...], axis=0, keepdims=True) * SCALE2)
            alpha = jnp.exp2(m_old - m_new)
            m_ref[slot] = m_new
            m_row = m_new[0:1]
            mx = ls = pv = None
            for b in range(blocks):
                p = jnp.exp2(s_ref[b * KEY_BLOCK:(b + 1) * KEY_BLOCK, :] * SCALE2 - m_row)
                ls = fold(ls, jnp.sum(p.reshape(KEY_BLOCK // 8, 8, tile_q), axis=0), jnp.add)
                mx = fold(mx, qk(b, next_chunks, next_q), jnp.maximum)
                vv = vbuf[chunks[b // per_chunk], :, (b % per_chunk) * KEY_BLOCK:(b % per_chunk + 1) * KEY_BLOCK]
                pv = fold(pv, jnp.dot(vv, p.astype(jnp.bfloat16), preferred_element_type=jnp.float32), jnp.add)
            mx_ref[...] = mx
            l_ref[slot] = l_ref[slot] * alpha + ls
            acc[slot] = acc[slot] * alpha[0:1] + pv

        def where_is(g):
            p = g // tiles
            t = g % tiles
            src = peer(block_index(p, t))
            hf = t % halves
            return p, t, src, hf

        def run(g, last):
            p, t, src, hf = where_is(g)
            g2 = jnp.minimum(g + 1, phases * tiles - 1)
            p2, t2, src2, hf2 = where_is(g2)

            if not last:
                @pl.when(jnp.logical_and(t2 == 0, p2 > 0))
                def _():
                    for c in range(2):
                        who = peer(2 * p2 + c)
                        k_copy(who, who).wait_recv()
                        v_copy(who, who).wait_recv()

                @pl.when(jnp.logical_and(p2 == 0, hf2 == 0))
                def _():
                    q_copy(src2, src2).wait_recv()

            step(src * halves + hf, [peer(2 * p), peer(2 * p + 1)], [peer(2 * p2), peer(2 * p2 + 1)], q_of(src2, hf2))
            return src, hf

        own_k.wait()
        own_v.wait()
        who = peer(1)
        k_copy(who, who).wait_recv()
        v_copy(who, who).wait_recv()
        first_q = q_of(me, 0)
        mx = None
        for b in range(blocks):
            mx = fold(mx, qk(b, [me, who], first_q), jnp.maximum)
        mx_ref[...] = mx

        def early_step(g, _):
            run(g, False)
            return 0

        lax.fori_loop(0, (phases - 1) * tiles, early_step, 0)

        for j in range(1, n):
            who = peer(j)
            nk_copy(who, who).wait_recv()
            nv_copy(who, who).wait_recv()

        def new_unit(src, hf, unit):
            slot = src * halves + hf
            q = q_of(src, hf)
            lane = lax.broadcasted_iota(jnp.int32, (KEY_BLOCK, tile_q), 1)
            diff = lane % rows - lax.broadcasted_iota(jnp.int32, (KEY_BLOCK, tile_q), 0)
            mx = None
            for b in range(NEW_UNIT):
                kb = unit * NEW_UNIT + b
                s = lax.dot_general(nkbuf[kb], q, (((1,), (1,)), ((), ())), preferred_element_type=jnp.float32)
                s = jnp.where(diff >= (kb - src) * rows, s, NEG_INF)
                s2_ref[b * KEY_BLOCK:(b + 1) * KEY_BLOCK, :] = s
                mx = fold(mx, jnp.max(s.reshape(KEY_BLOCK // 8, 8, tile_q), axis=0), jnp.maximum)
            m_old = m_ref[slot]
            m_new = jnp.maximum(m_old, jnp.max(mx, axis=0, keepdims=True) * SCALE2)
            alpha = jnp.exp2(m_old - m_new)
            m_ref[slot] = m_new
            m_row = m_new[0:1]
            ls = pv = None
            for b in range(NEW_UNIT):
                p = jnp.exp2(s2_ref[b * KEY_BLOCK:(b + 1) * KEY_BLOCK, :] * SCALE2 - m_row)
                ls = fold(ls, jnp.sum(p.reshape(KEY_BLOCK // 8, 8, tile_q), axis=0), jnp.add)
                pv = fold(pv, jnp.dot(nvbuf[unit * NEW_UNIT + b], p.astype(jnp.bfloat16), preferred_element_type=jnp.float32), jnp.add)
            l_ref[slot] = l_ref[slot] * alpha + ls
            acc[slot] = acc[slot] * alpha[0:1] + pv

        for unit in range(n // NEW_UNIT):
            def unit_step(i, _, unit=unit):
                t = i + unit * NEW_UNIT * halves
                new_unit(t // halves, t % halves, unit)
                return 0

            lax.fori_loop(0, (n - unit * NEW_UNIT) * halves, unit_step, 0)

        def late_step(g, _):
            src, hf = run(g, True)
            slot = src * halves + hf
            o = acc[slot] / jnp.sum(l_ref[slot], axis=0, keepdims=True)
            o = o.T.astype(jnp.bfloat16)
            for i in range(tile_q // rows):
                osend[src, hf * (tile_q // rows) + i] = o[i * rows:(i + 1) * rows]

            @pl.when(jnp.logical_and(hf == halves - 1, g < phases * tiles - 1))
            def _():
                o_copy(src, me).start()

            return 0

        lax.fori_loop((phases - 1) * tiles, phases * tiles, late_step, 0)
        obuf[me] = osend[me]

        for j in range(n - 1, 0, -1):
            who = peer(j)
            o_copy(who, who).wait_recv()
        o_all = jnp.concatenate([obuf[i, g] for i in range(n) for g in range(group)], axis=-1)
        h_ref[...] = o_all
        n_out = n

        def out_tile(t, _):
            slot = t % W_SLOTS
            w_copy(wo, t, slot).wait()
            y = jnp.dot(h_ref[...], wbuf[slot], preferred_element_type=jnp.float32)
            cols = pl.ds(pl.multiple_of(t * W_COLS, W_COLS), W_COLS)
            out_ref[:, cols] = (x_ref[:, cols].astype(jnp.float32) + y).astype(jnp.bfloat16)

            @pl.when(t < n_out - W_SLOTS)
            def _():
                w_copy(wo, t + W_SLOTS, slot).start()

            return 0

        lax.fori_loop(0, n_out, out_tile, 0)

        for j in range(1, n):
            who = peer(j)
            for copy in (k_copy, v_copy, q_copy, nk_copy, nv_copy, o_copy):
                copy(who, me).wait_send()

    return kernel


def solution(mesh):
    n = mesh.shape['cp']
    row_spec = P(('dp', 'cp'), None)
    cache_spec = P(('dp', 'cp'), None, None)
    whole = P()

    def device_step(x_rows, k_cache, v_cache, ln_gain, w_q, w_k, w_v, w_o, q_gain, k_gain):
        rows, hidden = x_rows.shape
        cache_rows, kv_heads, _ = k_cache.shape
        group = w_q.shape[1] // HEAD_DIM // kv_heads
        q_rows = rows * group
        tile_q = 512
        tiles = n * q_rows // tile_q
        positions = cache_rows * n + lax.axis_index('cp') * rows + jnp.arange(rows)
        cos_tab, sin_tab = rope_tables(positions)
        k_heads = jnp.transpose(k_cache, (1, 0, 2))
        v_heads = jnp.transpose(v_cache, (1, 2, 0))
        bf16 = jnp.bfloat16
        f32 = jnp.float32
        vmem = pl.BlockSpec(memory_space=pltpu.VMEM)
        hbm = pl.BlockSpec(memory_space=pl.ANY)
        dma = pltpu.SemaphoreType.DMA
        call = pl.pallas_call(
            make_kernel(n, rows, cache_rows, group),
            out_shape=(jax.ShapeDtypeStruct((rows, hidden), bf16),
                       jax.ShapeDtypeStruct((kv_heads, rows, HEAD_DIM), bf16),
                       jax.ShapeDtypeStruct((kv_heads, rows, HEAD_DIM), bf16)),
            in_specs=[vmem] * 6 + [hbm] * 6,
            out_specs=[vmem] * 3,
            scratch_shapes=[
                pltpu.VMEM((rows, hidden), bf16),
                pltpu.VMEM((W_SLOTS, hidden, W_COLS), bf16),
                pltpu.VMEM((n, cache_rows, HEAD_DIM), bf16),
                pltpu.VMEM((n, HEAD_DIM, cache_rows), bf16),
                pltpu.VMEM((n, q_rows, HEAD_DIM), bf16),
                pltpu.VMEM((n, q_rows, HEAD_DIM), bf16),
                pltpu.VMEM((n, rows, HEAD_DIM), bf16),
                pltpu.VMEM((n, HEAD_DIM, rows), bf16),
                pltpu.VMEM((n, HEAD_DIM, rows), bf16),
                pltpu.VMEM((n, group, rows, HEAD_DIM), bf16),
                pltpu.VMEM((n, group, rows, HEAD_DIM), bf16),
                pltpu.VMEM((2 * cache_rows, tile_q), f32),
                pltpu.VMEM((NEW_UNIT * KEY_BLOCK, tile_q), f32),
                pltpu.VMEM((tiles, HEAD_DIM, tile_q), f32),
                pltpu.VMEM((tiles, 8, tile_q), f32),
                pltpu.VMEM((tiles, 8, tile_q), f32),
                pltpu.VMEM((8, tile_q), f32),
                dma((W_SLOTS,)), dma((2,)),
            ] + [dma((n,))] * 12,
            compiler_params=pltpu.CompilerParams(collective_id=0, has_side_effects=True, vmem_limit_bytes=67043328),
        )
        out, k_new, v_new = call(x_rows, ln_gain[None, :], q_gain[None, :], k_gain[None, :], cos_tab, sin_tab,
                                 k_heads, v_heads, w_q, w_k, w_v, w_o)
        return out, jnp.transpose(k_new, (1, 0, 2)), jnp.transpose(v_new, (1, 0, 2))

    return jax.shard_map(device_step, mesh=mesh, in_specs=(row_spec, cache_spec, cache_spec, whole, whole, whole, whole, whole, whole, whole), out_specs=(row_spec, cache_spec, cache_spec), check_vma=False)
```

time: 1280 us -> 226 us (0.18)
  matrix products: 492 us -> 0 us
  waiting for transfers between devices: 428 us -> 0 us
  other arithmetic: 237 us -> 1.39 us
  Pallas kernels: 0 us -> 204 us
  local copies, waits for them, and re-layouts: 69.3 us -> 20.1 us
  blocking collectives: 20.3 us -> 0 us
  between operations: 14.5 us -> 0.66 us
    dot_general x36 -> x0, matrix products: 492 us -> none  [the longest x16 251 us: partial_attend(): jnp.einsum('krgs,skd->krgd', weights.astype(jnp.bfloat16), vals, preferre...]
    all_to_all x1 -> x0, waiting for transfers between devices: 348 us -> none  [device_step(): lax.all_to_all(piece, 'cp', 0, 0, tiled=True)]
    reduce_sum x22 -> x0, other arithmetic: 219 us -> none  [the longest x16 185 us: partial_attend(): return (peak, jnp.sum(weights, axis=-1), weighted)]
    pallas_call x0 -> x1, Pallas kernels: none -> 204 us  [device_step(): call(x_rows, ln_gain[None, :], q_gain[None, :], k_gain[None, :], cos_tab,...]
    all_gather x3 -> x0, waiting for transfers between devices: 80.5 us -> none  [the longest x1 80.5 us: device_step(): every_q = lax.all_gather(q_grp, 'cp')]
    dynamic_slice x32 -> x0, local copies, waits for them, and re-layouts: 38.4 us -> none  [device_step(): lax.map(block_work, (every_q, every_k, every_v, jnp.arange(cp_size)))]
    all_to_all x2 -> x0, blocking collectives: 20.3 us -> none  [device_step(): lax.all_to_all(piece, 'cp', 0, 0, tiled=True)]
  transfers between devices with their start and end apart: 4 -> 0, of which waited for: 2 -> 0; matrix products, arithmetic and copies ran while one was open for 6% -> 0% of each run, Pallas kernels for 0% -> 0%
where the time goes in v1:
time: 226 us
  Pallas kernels  204 us (90%)
  local copies, waits for them, and re-layouts  20.1 us (9%)
    pallas_call x1, Pallas kernels, device_step(): call(x_rows, ln_gain[None, :], q_gain[None, :], k_gain[None, :], cos_tab,...  204 us
    unnamed x5, local copies, waits for them, and re-layouts  18.8 us

profile of v1, /device:TPU:113, one launch (start us, length us, event | category | flops | bytes accessed | tf_op | source)
XLA Modules:
  0.0 225.8 jit_solution(11529200416350445651)
XLA Ops:
  0.7 1.3 broadcast_in_dim.11.gain_ref
  2.0 0.5 fusion
  2.5 0.8 pad_maximum_fusion
  3.4 4.7 %copy.18 = bf16[2048,8,128]{2,0,1:T(8,128)(2,1)} copy(bf16[2048,8,128]{2,1,0:T(8,128)(2,1)} %param.11) | data formatting | bytes 8388608 | tf_op args[1]
  8.0 6.7 %copy.14 = bf16[2048,8,128]{0,2,1:T(8,128)(2,1)} copy(bf16[2048,8,128]{2,1,0:T(8,128)(2,1)} %param.12) | data formatting | bytes 8388608 | tf_op args[2]
  14.7 203.6 %shard_map.121 = (bf16[256,4096]{1,0:T(8,128)(2,1)}, bf16[8,256,128]{2,1,0:T(8,128)(2,1)}, bf16[8,256,128]{2,1,0:T(8,128)(2,1)}) custom-call(bf16[256,4096]{1,0:T(8,128)(2,1)} %x_ref.1, bf16[1,4096]{1,0:T(2,128)(2,1)} %broadcast_in_dim.11.gain_ref, bf16[1,128]{1,0:T(2,128)(2,1)} %bitcast.12, bf16[1,128]{1,0:T(2,128)(2,1)} %bitcast.13, ...), custom_call_target="tpu_custom_call" | custom-call | tf_op jit(solution)/shard_map/pallas_call | solution.py:433
  218.3 2.2 copy.15
  220.5 2.2 copy.16
  222.7 3.1 %copy.20 = bf16[256,4096]{1,0:T(8,128)(2,1)} copy(bf16[256,4096]{1,0:T(8,128)(2,1)} %get-tuple-element.20) | data formatting | bytes 4194304
  (2 shorter events, 0.0 us)

commit v2 on v1

v2 whole, which is shorter than its diff:
```python
import functools

import jax
import jax.numpy as jnp
from jax import lax
from jax.experimental import pallas as pl
from jax.experimental.pallas import tpu as pltpu
from jax.sharding import PartitionSpec as P

HEAD_DIM = 128
ROPE_THETA = 1.0e6
NORM_EPS = 1.0e-6
SCALE2 = HEAD_DIM ** -0.5 * 1.4426950408889634
KEY_BLOCK = 256
NEW_UNIT = 4
W_SLOTS = 3
W_COLS = 512
RELAY = 256
MESH = pl.DeviceIdType.MESH
NEG_INF = float('-inf')


def rope_tables(positions):
    half = HEAD_DIM // 2
    inv_freq = ROPE_THETA ** (-jnp.arange(half, dtype=jnp.float32) * (2.0 / HEAD_DIM))
    angles = positions.astype(jnp.float32)[:, None] * inv_freq[None, :]
    cos_tab = jnp.cos(angles)
    sin_tab = jnp.sin(angles)
    return jnp.concatenate([cos_tab, cos_tab], axis=-1), jnp.concatenate([-sin_tab, sin_tab], axis=-1)


def ring_order(n):
    chips = n // 2
    order = [(0, 0), (0, 1)]
    for d in range(1, chips // 2 + 1):
        if 2 * d == chips:
            order += [(d, 0), (d, 1)]
        else:
            order += [(d, 0), (chips - d, 0), (d, 1), (chips - d, 1)]
    return order


def make_kernel(n, rows, cache_rows, group):
    order = ring_order(n)
    chips = n // 2
    qcols = group * HEAD_DIM
    tile_q = 512
    halves = rows * group // tile_q
    tiles = n * halves
    phases = n // 2
    blocks = 2 * cache_rows // KEY_BLOCK
    per_chunk = cache_rows // KEY_BLOCK
    kv_per_tile = W_COLS // HEAD_DIM

    def kernel(x_ref, gain_ref, qg_ref, kg_ref, cos_ref, sin_ref, kc_raw, vc_raw, wq, wk, wv, wo,
               out_ref, kn_ref, vn_ref,
               h_ref, wbuf, kc, vc, kbuf, vbuf, qsend, qbuf, nkbuf, nvsend, nvbuf,
               s_ref, s2_ref, acc, m_ref, l_ref, mx_ref, mx2_ref, raw,
               wsem, rawsem, sk, rk, sv, rv, sq, rq, snk, rnk, snv, rnv, so, ro):
        me = lax.axis_index('cp')
        chip = me // 2
        core = me % 2

        def peer(j):
            if isinstance(j, int):
                dc, fl = order[j]
            else:
                dc, fl = jnp.int32(0), jnp.int32(0)
                for i, (a, b) in enumerate(order):
                    dc = jnp.where(j == i, a, dc)
                    fl = jnp.where(j == i, b, fl)
            return ((chip + dc) % chips) * 2 + (core + fl) % 2

        def remote(src, dst, ssem, rsem, dev):
            return pltpu.make_async_remote_copy(src_ref=src, dst_ref=dst, send_sem=ssem, recv_sem=rsem,
                                                device_id={'cp': dev}, device_id_type=MESH)

        def k_copy(dev, who):
            return remote(kc.at[dev], kbuf.at[who], sk.at[dev], rk.at[who], dev)

        def v_copy(dev, who):
            return remote(vc.at[dev], vbuf.at[who], sv.at[dev], rv.at[who], dev)

        def q_copy(dev, who):
            return remote(qsend.at[dev], qbuf.at[who], sq.at[dev], rq.at[who], dev)

        def nk_copy(dev, who):
            return remote(kn_ref.at[dev], nkbuf.at[who], snk.at[dev], rnk.at[who], dev)

        def nv_copy(dev, who):
            return remote(nvsend.at[dev], nvbuf.at[who], snv.at[dev], rnv.at[who], dev)

        def o_copy(dev, who):
            return remote(qsend.at[dev], h_ref.at[:, pl.ds(pl.multiple_of(who * qcols, qcols), qcols)],
                          so.at[dev], ro.at[who], dev)

        def w_copy(src, col, slot):
            return pltpu.make_async_copy(src.at[:, pl.ds(pl.multiple_of(col * W_COLS, W_COLS), W_COLS)],
                                         wbuf.at[slot], wsem.at[slot])

        def q_dest(t):
            if isinstance(t, int):
                return peer(t + 2 if t < n - 2 else n - 1 - t)
            return peer(jnp.where(t < n - 2, t + 2, n - 1 - t))

        for t in range(W_SLOTS):
            w_copy(wq, q_dest(t), t).start()
        def raw_copy(src, r, slot):
            return pltpu.make_async_copy(src.at[pl.ds(pl.multiple_of(r * RELAY, RELAY), RELAY)],
                                         raw.at[slot], rawsem.at[slot])

        relays = cache_rows // RELAY
        for r in range(2):
            raw_copy(kc_raw, r, r).start()

        barrier = pltpu.get_barrier_semaphore()
        for j in range(1, n):
            pl.semaphore_signal(barrier, inc=1, device_id={'cp': peer(j)}, device_id_type=MESH)
        pl.semaphore_wait(barrier, n - 1)

        def relay_k(r, _):
            slot = r % 2
            raw_copy(kc_raw, r, slot).wait()
            for i in range(RELAY // 64):
                to = pl.ds(pl.multiple_of(r * RELAY + i * 64, 64), 64)
                kc[:, to, :] = jnp.swapaxes(raw[slot, i * 64:(i + 1) * 64], 0, 1)

            @pl.when(r < relays - 2)
            def _():
                raw_copy(kc_raw, r + 2, slot).start()

            return 0

        lax.fori_loop(0, relays, relay_k, 0)
        for r in range(2):
            raw_copy(vc_raw, r, r).start()
        for j in range(1, n // 2):
            k_copy(peer(j), me).start()
        kbuf[me] = kc[me]

        gain = gain_ref[...].astype(jnp.float32)[None, :]

        def norm_rows(r, _):
            sl = pl.ds(pl.multiple_of(r * 32, 32), 32)
            xw = x_ref[sl, :].astype(jnp.float32)
            ms = jnp.mean(xw * xw, axis=-1, keepdims=True)
            h_ref[sl, :] = (xw * lax.rsqrt(ms + NORM_EPS) * gain).astype(jnp.bfloat16)
            return 0

        lax.fori_loop(0, rows // 32, norm_rows, 0)

        def init_tile(t, _):
            acc[t] = jnp.zeros((HEAD_DIM, tile_q), jnp.float32)
            m_ref[t] = jnp.full((8, tile_q), NEG_INF, jnp.float32)
            l_ref[t] = jnp.zeros((8, tile_q), jnp.float32)
            return 0

        lax.fori_loop(0, tiles, init_tile, 0)

        def project(slot):
            return jnp.dot(h_ref[...], wbuf[slot], preferred_element_type=jnp.float32).astype(jnp.bfloat16)

        def norm_rope(raw, head_gain):
            val = raw.astype(jnp.float32)
            ms = jnp.mean(val * val, axis=-1, keepdims=True)
            val = val * lax.rsqrt(ms + NORM_EPS) * head_gain
            return (val * cos_ref[...] + pltpu.roll(val, HEAD_DIM // 2, 1) * sin_ref[...]).astype(jnp.bfloat16)

        q_gain = qg_ref[...].astype(jnp.float32)
        k_gain = kg_ref[...].astype(jnp.float32)
        k_tiles = n // kv_per_tile

        def relay_v(r, rslot):
            for i in range(RELAY // 128):
                to = pl.ds(pl.multiple_of(r * RELAY + i * 128, 128), 128)
                heads = jnp.swapaxes(raw[rslot, i * 128:(i + 1) * 128], 0, 1)
                for g in range(n):
                    vc[g, :, to] = heads[g].T

        assert relays == n
        first_k, first_v, first_o = n, n + k_tiles, n + 2 * k_tiles

        def prefetch(i, lo, hi):
            slot = i % W_SLOTS
            if lo < first_k:
                @pl.when(i < first_k)
                def _():
                    w_copy(wq, q_dest(i), slot).start()

            for j in range(max(lo, first_k), min(hi, first_o)):
                @pl.when(i == j)
                def _(j=j):
                    src, first = (wk, first_k) if j < first_v else (wv, first_v)
                    w_copy(src, j - first, slot).start()

            if hi > first_o:
                @pl.when(jnp.logical_and(i >= first_o, i < first_o + n))
                def _():
                    w_copy(wo, i - first_o, slot).start()

        def q_tile(t, _):
            slot = t % W_SLOTS
            dest = q_dest(t)
            w_copy(wq, dest, slot).wait()
            rslot = t % 2
            raw_copy(vc_raw, t, rslot).wait()
            y = project(slot)
            relay_v(t, rslot)
            for g in range(group):
                cols = slice(g * HEAD_DIM, (g + 1) * HEAD_DIM)
                qsend[dest, :, cols] = norm_rope(y[:, cols], q_gain)

            @pl.when(t < relays - 2)
            def _():
                raw_copy(vc_raw, t + 2, rslot).start()

            prefetch(t + W_SLOTS, W_SLOTS, n + W_SLOTS)

            @pl.when(t < n - 1)
            def _():
                q_copy(dest, me).start()

            return 0

        lax.fori_loop(0, n, q_tile, 0)
        for j in range(1, n // 2):
            v_copy(peer(j), me).start()
        for j in range(n // 2, n - 2):
            k_copy(peer(j), me).start()
            v_copy(peer(j), me).start()
        qbuf[me] = qsend[me]
        vbuf[me] = vc[me]

        def k_tile(t, _):
            slot = (first_k + t) % W_SLOTS
            w_copy(wk, t, slot).wait()
            y = project(slot)
            for g in range(kv_per_tile):
                kn_ref[t * kv_per_tile + g] = norm_rope(y[:, g * HEAD_DIM:(g + 1) * HEAD_DIM], k_gain)
            prefetch(first_k + t + W_SLOTS, first_k + W_SLOTS, first_v + W_SLOTS)
            return 0

        lax.fori_loop(0, k_tiles, k_tile, 0)
        nkbuf[me] = kn_ref[me]

        def v_tile(t, _):
            slot = (first_v + t) % W_SLOTS
            w_copy(wv, t, slot).wait()
            y = project(slot)
            for g in range(kv_per_tile):
                val = y[:, g * HEAD_DIM:(g + 1) * HEAD_DIM]
                vn_ref[t * kv_per_tile + g] = val
                nvsend[t * kv_per_tile + g] = val.T
            prefetch(first_v + t + W_SLOTS, first_v + W_SLOTS, first_o + W_SLOTS)
            return 0

        lax.fori_loop(0, k_tiles, v_tile, 0)
        nvbuf[me] = nvsend[me]

        for j in range(1, n):
            nk_copy(peer(j), me).start()
            nv_copy(peer(j), me).start()
        for j in range(n - 2, n):
            k_copy(peer(j), me).start()
            v_copy(peer(j), me).start()

        def q_of(src, hf):
            per = tile_q // rows
            return jnp.concatenate(
                [qbuf[src, :, pl.ds(pl.multiple_of((hf * per + i) * HEAD_DIM, HEAD_DIM), HEAD_DIM)] for i in range(per)],
                axis=0)

        def qk(b, chunks, q):
            kk = kbuf[chunks[b // per_chunk], (b % per_chunk) * KEY_BLOCK:(b % per_chunk + 1) * KEY_BLOCK, :]
            s = lax.dot_general(kk, q, (((1,), (1,)), ((), ())), preferred_element_type=jnp.float32)
            s_ref[b * KEY_BLOCK:(b + 1) * KEY_BLOCK, :] = s
            return jnp.max(s.reshape(KEY_BLOCK // 8, 8, tile_q), axis=0)

        def fold(total, term, op):
            return term if total is None else op(total, term)

        def step(slot, chunks, next_chunks, next_q):
            m_old = m_ref[slot]
            m_new = jnp.maximum(m_old, jnp.max(mx_ref[...], axis=0, keepdims=True) * SCALE2)
            alpha = jnp.exp2(m_old - m_new)
            m_ref[slot] = m_new
            m_row = m_new[0:1]
            mx = ls = pv = None
            for b in range(blocks):
                p = jnp.exp2(s_ref[b * KEY_BLOCK:(b + 1) * KEY_BLOCK, :] * SCALE2 - m_row)
                ls = fold(ls, jnp.sum(p.reshape(KEY_BLOCK // 8, 8, tile_q), axis=0), jnp.add)
                mx = fold(mx, qk(b, next_chunks, next_q), jnp.maximum)
                vv = vbuf[chunks[b // per_chunk], :, (b % per_chunk) * KEY_BLOCK:(b % per_chunk + 1) * KEY_BLOCK]
                pv = fold(pv, jnp.dot(vv, p.astype(jnp.bfloat16), preferred_element_type=jnp.float32), jnp.add)
            mx_ref[...] = mx
            l_ref[slot] = l_ref[slot] * alpha + ls
            acc[slot] = acc[slot] * alpha[0:1] + pv

        pairs = [[peer(2 * p), peer(2 * p + 1)] for p in range(phases)]

        def block_of(p, t):
            i = t // halves
            return peer(n - 1 - i if p == phases - 1 else i)

        def block_after(p, t):
            if p == phases - 1:
                return block_of(p, jnp.minimum(t, tiles - 1))
            return jnp.where(t < tiles, block_of(p, jnp.minimum(t, tiles - 1)), block_of(p + 1, 0))

        def run_phase(p, after):
            def one(t, carry):
                src, nxt = carry
                if p < phases - 1:
                    @pl.when(t == tiles - 1)
                    def _():
                        for who in pairs[p + 1]:
                            k_copy(who, who).wait_recv()
                            v_copy(who, who).wait_recv()

                if p == 0:
                    @pl.when(jnp.logical_and((t + 1) % halves == 0, t < tiles - 1))
                    def _():
                        q_copy(nxt, nxt).wait_recv()

                later = pairs[min(p + 1, phases - 1)]
                next_chunks = [jnp.where(t == tiles - 1, b, a) for a, b in zip(pairs[p], later)]
                hf = t % halves
                step(src * halves + hf, pairs[p], next_chunks, q_of(nxt, (t + 1) % halves))
                after(t, src, hf)
                return nxt, block_after(p, t + 2)

            lax.fori_loop(0, tiles, one, (block_of(p, jnp.int32(0)), block_of(p, jnp.int32(1))))

        who = peer(1)
        k_copy(who, who).wait_recv()
        v_copy(who, who).wait_recv()
        first_q = q_of(me, 0)
        mx = None
        for b in range(blocks):
            mx = fold(mx, qk(b, [me, who], first_q), jnp.maximum)
        mx_ref[...] = mx

        for p in range(phases - 1):
            run_phase(p, lambda t, src, hf: None)

        for j in range(1, n):
            who = peer(j)
            nk_copy(who, who).wait_recv()
            nv_copy(who, who).wait_recv()

        new_steps = n + n - NEW_UNIT
        assert n == 2 * NEW_UNIT

        def new_place(k):
            unit = k // n
            return k - unit * (n - NEW_UNIT), unit

        def new_scores(src, unit, hf, b, q):
            lane = lax.broadcasted_iota(jnp.int32, (KEY_BLOCK, tile_q), 1)
            diff = lane % rows - lax.broadcasted_iota(jnp.int32, (KEY_BLOCK, tile_q), 0)
            kb = unit * NEW_UNIT + b
            s = lax.dot_general(nkbuf[kb], q, (((1,), (1,)), ((), ())), preferred_element_type=jnp.float32)
            s = jnp.where(diff >= (kb - src) * rows, s, NEG_INF)
            s2_ref[hf, b * KEY_BLOCK:(b + 1) * KEY_BLOCK, :] = s
            return jnp.max(s.reshape(KEY_BLOCK // 8, 8, tile_q), axis=0)

        def new_step(k, _):
            src, unit = new_place(k)
            src2, unit2 = new_place(jnp.minimum(k + 1, new_steps - 1))
            qs = [q_of(src2, hf) for hf in range(halves)]
            m_rows, alphas = [], []
            for hf in range(halves):
                m_old = m_ref[src * halves + hf]
                m_new = jnp.maximum(m_old, jnp.max(mx2_ref[hf], axis=0, keepdims=True) * SCALE2)
                alphas.append(jnp.exp2(m_old - m_new))
                m_ref[src * halves + hf] = m_new
                m_rows.append(m_new[0:1])
            mx, ls, pv = [None] * halves, [None] * halves, [None] * halves
            for b in range(NEW_UNIT):
                for hf in range(halves):
                    p = jnp.exp2(s2_ref[hf, b * KEY_BLOCK:(b + 1) * KEY_BLOCK, :] * SCALE2 - m_rows[hf])
                    ls[hf] = fold(ls[hf], jnp.sum(p.reshape(KEY_BLOCK // 8, 8, tile_q), axis=0), jnp.add)
                    mx[hf] = fold(mx[hf], new_scores(src2, unit2, hf, b, qs[hf]), jnp.maximum)
                    pv[hf] = fold(pv[hf], jnp.dot(nvbuf[unit * NEW_UNIT + b], p.astype(jnp.bfloat16),
                                                  preferred_element_type=jnp.float32), jnp.add)
            for hf in range(halves):
                slot = src * halves + hf
                mx2_ref[hf] = mx[hf]
                l_ref[slot] = l_ref[slot] * alphas[hf] + ls[hf]
                acc[slot] = acc[slot] * alphas[hf][0:1] + pv[hf]
            return 0

        for hf in range(halves):
            mx = None
            q = q_of(0, hf)
            for b in range(NEW_UNIT):
                mx = fold(mx, new_scores(0, 0, hf, b, q), jnp.maximum)
            mx2_ref[hf] = mx
        lax.fori_loop(0, new_steps, new_step, 0)

        for j in range(1, n):
            q_copy(peer(j), me).wait_send()

        def send_home(t, src, hf):
            slot = src * halves + hf
            o = acc[slot] / jnp.sum(l_ref[slot], axis=0, keepdims=True)
            o = o.T.astype(jnp.bfloat16)
            per = tile_q // rows
            for i in range(per):
                cols = pl.ds(pl.multiple_of((hf * per + i) * HEAD_DIM, HEAD_DIM), HEAD_DIM)
                qsend[src, :, cols] = o[i * rows:(i + 1) * rows]

            @pl.when(jnp.logical_and(hf == halves - 1, t < tiles - 1))
            def _():
                o_copy(src, me).start()

        run_phase(phases - 1, send_home)
        h_ref[:, pl.ds(pl.multiple_of(me * qcols, qcols), qcols)] = qsend[me]

        for j in range(n - 1, 0, -1):
            who = peer(j)
            o_copy(who, who).wait_recv()

        def out_tile(t, _):
            slot = (first_o + t) % W_SLOTS
            w_copy(wo, t, slot).wait()
            y = jnp.dot(h_ref[...], wbuf[slot], preferred_element_type=jnp.float32)
            cols = pl.ds(pl.multiple_of(t * W_COLS, W_COLS), W_COLS)
            out_ref[:, cols] = (x_ref[:, cols].astype(jnp.float32) + y).astype(jnp.bfloat16)
            prefetch(first_o + t + W_SLOTS, first_o + W_SLOTS, first_o + n + W_SLOTS)
            return 0

        lax.fori_loop(0, n, out_tile, 0)

        for j in range(1, n):
            who = peer(j)
            for copy in (k_copy, v_copy, nk_copy, nv_copy, o_copy):
                copy(who, me).wait_send()

    return kernel


def finish(out_in, k_in, v_in, out_ref, k_ref, v_ref, rows_buf, heads_buf, turned_buf, isem, osem):
    parts = rows_buf.shape[0]
    part = rows_buf.shape[1]
    rows_in = [pltpu.make_async_copy(out_in.at[pl.ds(i * part, part)], rows_buf.at[i], isem.at[i]) for i in range(parts)]
    rows_out = [pltpu.make_async_copy(rows_buf.at[i], out_ref.at[pl.ds(i * part, part)], osem.at[i]) for i in range(parts)]
    heads_in = [pltpu.make_async_copy(src, heads_buf.at[i], isem.at[parts + i]) for i, src in enumerate((k_in, v_in))]
    turned_out = [pltpu.make_async_copy(turned_buf.at[i], dst, osem.at[parts + i]) for i, dst in enumerate((k_ref, v_ref))]
    for copy in heads_in + rows_in:
        copy.start()
    for i in range(2):
        heads_in[i].wait()
        for r in range(0, turned_buf.shape[1], 64):
            turned_buf[i, r:r + 64] = jnp.swapaxes(heads_buf[i, :, r:r + 64], 0, 1)
        turned_out[i].start()
    for i in range(parts):
        rows_in[i].wait()
        rows_out[i].start()
    for copy in turned_out + rows_out:
        copy.wait()


def solution(mesh):
    n = mesh.shape['cp']
    row_spec = P(('dp', 'cp'), None)
    cache_spec = P(('dp', 'cp'), None, None)
    whole = P()

    def device_step(x_rows, k_cache, v_cache, ln_gain, w_q, w_k, w_v, w_o, q_gain, k_gain):
        rows, hidden = x_rows.shape
        cache_rows, kv_heads, _ = k_cache.shape
        group = w_q.shape[1] // HEAD_DIM // kv_heads
        q_rows = rows * group
        tile_q = 512
        tiles = n * q_rows // tile_q
        positions = cache_rows * n + lax.axis_index('cp') * rows + jnp.arange(rows)
        cos_tab, sin_tab = rope_tables(positions)
        bf16 = jnp.bfloat16
        f32 = jnp.float32
        vmem = pl.BlockSpec(memory_space=pltpu.VMEM)
        hbm = pl.BlockSpec(memory_space=pl.ANY)
        dma = pltpu.SemaphoreType.DMA
        call = pl.pallas_call(
            make_kernel(n, rows, cache_rows, group),
            out_shape=(jax.ShapeDtypeStruct((rows, hidden), bf16),
                       jax.ShapeDtypeStruct((kv_heads, rows, HEAD_DIM), bf16),
                       jax.ShapeDtypeStruct((kv_heads, rows, HEAD_DIM), bf16)),
            in_specs=[vmem] * 6 + [hbm] * 6,
            out_specs=[vmem] * 3,
            scratch_shapes=[
                pltpu.VMEM((rows, hidden), bf16),
                pltpu.VMEM((W_SLOTS, hidden, W_COLS), bf16),
                pltpu.VMEM((n, cache_rows, HEAD_DIM), bf16),
                pltpu.VMEM((n, HEAD_DIM, cache_rows), bf16),
                pltpu.VMEM((n, cache_rows, HEAD_DIM), bf16),
                pltpu.VMEM((n, HEAD_DIM, cache_rows), bf16),
                pltpu.VMEM((n, rows, group * HEAD_DIM), bf16),
                pltpu.VMEM((n, rows, group * HEAD_DIM), bf16),
                pltpu.VMEM((n, rows, HEAD_DIM), bf16),
                pltpu.VMEM((n, HEAD_DIM, rows), bf16),
                pltpu.VMEM((n, HEAD_DIM, rows), bf16),
                pltpu.VMEM((2 * cache_rows, tile_q), f32),
                pltpu.VMEM((q_rows // tile_q, NEW_UNIT * KEY_BLOCK, tile_q), f32),
                pltpu.VMEM((tiles, HEAD_DIM, tile_q), f32),
                pltpu.VMEM((tiles, 8, tile_q), f32),
                pltpu.VMEM((tiles, 8, tile_q), f32),
                pltpu.VMEM((8, tile_q), f32),
                pltpu.VMEM((q_rows // tile_q, 8, tile_q), f32),
                pltpu.VMEM((2, RELAY, kv_heads, HEAD_DIM), bf16),
                dma((W_SLOTS,)), dma((2,)),
            ] + [dma((n,))] * 12,
            compiler_params=pltpu.CompilerParams(collective_id=0, has_side_effects=True, vmem_limit_bytes=67043328),
        )
        out, k_new, v_new = call(x_rows, ln_gain, q_gain[None, :], k_gain[None, :], cos_tab, sin_tab,
                                 k_cache, v_cache, w_q, w_k, w_v, w_o)
        parts = 4
        return pl.pallas_call(
            finish,
            out_shape=(jax.ShapeDtypeStruct((rows, hidden), bf16),
                       jax.ShapeDtypeStruct((rows, kv_heads, HEAD_DIM), bf16),
                       jax.ShapeDtypeStruct((rows, kv_heads, HEAD_DIM), bf16)),
            in_specs=[hbm] * 3,
            out_specs=[hbm] * 3,
            scratch_shapes=[pltpu.VMEM((parts, rows // parts, hidden), bf16),
                            pltpu.VMEM((2, kv_heads, rows, HEAD_DIM), bf16),
                            pltpu.VMEM((2, rows, kv_heads, HEAD_DIM), bf16),
                            dma((parts + 2,)), dma((parts + 2,))],
        )(out, k_new, v_new)

    return jax.shard_map(device_step, mesh=mesh, in_specs=(row_spec, cache_spec, cache_spec, whole, whole, whole, whole, whole, whole, whole), out_specs=(row_spec, cache_spec, cache_spec), check_vma=False)
```

time: 226 us -> 210 us (0.929)
  local copies, waits for them, and re-layouts: 20.1 us -> 0 us
  Pallas kernels: 204 us -> 207 us
    unnamed x5 -> x0, local copies, waits for them, and re-layouts: 18.8 us -> none
    pallas_call x1 -> x2, Pallas kernels: 204 us -> 207 us  [the longest x1 204 us: device_step(): call(x_rows, ln_gain, q_gain[None, :], k_gain[None, :], cos_tab, sin_tab,...]
where the time goes in v2:
time: 210 us; the launch traced here: 209 us
  Pallas kernels  207 us (99%)
    pallas_call x1, Pallas kernels, device_step(): call(x_rows, ln_gain, q_gain[None, :], k_gain[None, :], cos_tab, sin_tab,...  204 us

profile of v2, /device:TPU:113, one launch (start us, length us, event | category | flops | bytes accessed | tf_op | source)
XLA Modules:
  0.0 209.5 jit_solution(8706430543303264177)
XLA Ops:
  0.7 0.5 fusion
  1.2 0.8 pad_maximum_fusion
  2.0 204.3 %shard_map.121 = (bf16[256,4096]{1,0:T(8,128)(2,1)}, bf16[8,256,128]{2,1,0:T(8,128)(2,1)}, bf16[8,256,128]{2,1,0:T(8,128)(2,1)}) custom-call(bf16[256,4096]{1,0:T(8,128)(2,1)} %x_ref.1, bf16[4096]{0:T(1024)(128)(2,1)} %gain_ref.1, bf16[1,128]{1,0:T(2,128)(2,1)} %bitcast.2, bf16[1,128]{1,0:T(2,128)(2,1)} %bitcast.3, f32[256,128]{1,0:T(8,128)} %get-tuple-element.12.cos_ref, ...), custom_call_target="tpu_custom_call" | custom-call | tf_op jit(solution)/shard_map/pallas_call | solution.py:515
  206.3 3.0 %shard_map.122 = (bf16[256,4096]{1,0:T(8,128)(2,1)}, bf16[256,8,128]{2,1,0:T(8,128)(2,1)}, bf16[256,8,128]{2,1,0:T(8,128)(2,1)}) custom-call(bf16[256,4096]{1,0:T(8,128)(2,1)} %get-tuple-element.6.out_in, bf16[8,256,128]{2,1,0:T(8,128)(2,1)} %get-tuple-element.7.k_in, bf16[8,256,128]{2,1,0:T(8,128)(2,1)} %get-tuple-element.8.v_in), custom_call_target="tpu_custom_call" | custom-call | tf_op jit(solution)/shard_map/pallas_call | solution.py:518
  (2 shorter events, 0.0 us)
